TPU v7x, 32 devices: a whole 2x2x4 slice. The times are simulated.
32 devices in a mesh: dm: 4 (over z), tm: 8 (over y, x, core).
Axes of the slice: x: 2, y: 2, z: 4, core: 2. Of those that a mesh axis runs over, the one named last changes fastest.
Arguments:
- dispersed: float32 [1024, 8192], P('dm', 'tm')
- widths: int32 [4], replicated, may hold values from 1 to 129, as said below
Outputs:
- snr: bfloat16 [4, 1024, 8192], P(None, 'dm', 'tm')
- peaks: float32 [4, 1024], P(None, 'dm')
Inputs may be any that keep to these rules, and one draw needn't show every extreme that they name: `widths`: at least one width equals 129.
All inputs are finite; a program needn't handle non-finite values.
Results may differ from a plain program's by a relative error of at most 0.001.
Values sent between devices are 32-bit elements; how exact they have to be, the bound alone decides.
A program may use at most 64 MiB of HBM per device.

v0:
```python
import jax
import jax.numpy as jnp
from jax import lax
from jax.sharding import PartitionSpec as P

HALF = 128


eps_value = 1e-06


def with_halo(x, sides, width):
    for axis, dim in sides:
        peers, length = (lax.axis_size(axis), x.shape[dim])
        up = [(i, (i + 1) % peers) for i in range(peers - 1)]
        down = [(j, i) for i, j in up]
        last = lax.slice_in_dim(x, length - width, length, axis=dim)
        leading = lax.slice_in_dim(x, 0, width, axis=dim)
        before = lax.ppermute(last, axis, up)
        after = lax.ppermute(leading, axis, down)
        x = jnp.concatenate([before, x, after], axis=dim)
    return x


def from_behind(block, axis, distance):
    devices = range(lax.axis_size(axis))
    route = [(i - distance, i) for i in devices if i - distance in devices]
    return lax.ppermute(block, axis, route)


def band_table(span_list, block_len):
    column_idx = jnp.arange(span_list.shape[0] * block_len, dtype=jnp.int32)
    offsets = column_idx % block_len
    reaches = jnp.repeat(span_list, block_len)
    row_idx = jnp.arange(2 * block_len, dtype=jnp.int32)[:, None]
    inside = (row_idx >= offsets[None, :]) & (row_idx < offsets[None, :] + reaches[None, :])
    return inside.astype(jnp.float32)


def window_sum(extended, length, band_matrix, block_len):
    row_count = extended.shape[0]
    block_count = length // block_len
    blocks = extended.reshape(row_count, block_count + 1, block_len)
    paired = jnp.concatenate([blocks[:, :-1], blocks[:, 1:]], axis=2)
    return jnp.einsum("rbs,sk->rbk", paired, band_matrix, precision=lax.Precision.HIGHEST)


def boxcar(extended, length, band_matrix, inverse, block_len):
    row_count = extended.shape[0]
    moving = window_sum(extended, length, band_matrix, block_len)
    moving = moving.reshape(row_count, length // block_len, inverse.shape[0], block_len)
    moving = jnp.transpose(moving, (2, 0, 1, 3)).reshape(inverse.shape[0], row_count, length)
    return moving * inverse[:, None, None]


def body(dispersed, widths):
    row_count, length = dispersed.shape
    block_len = 2 * HALF
    total_len = length * lax.axis_size("tm")
    offset = lax.axis_index("tm") * length
    ma_band = band_table(jnp.full((1,), 2 * HALF + 1, jnp.int32), block_len)
    box_band = band_table(widths, block_len)
    inverse = 1.0 / jnp.sqrt(widths.astype(jnp.float32))

    def counts_at(first_pos, size_len):
        positions = first_pos + jnp.arange(size_len, dtype=jnp.int32)
        counts = (
            jnp.minimum(positions + HALF, total_len - 1) - jnp.maximum(positions - HALF, 0) + 1
        ).astype(jnp.float32)
        inside = (positions >= 0) & (positions < total_len)
        return (counts, inside)

    local_counts = counts_at(offset, length)[0]
    extended = with_halo(dispersed, (("tm", 1),), 2 * HALF)
    wide_counts, inside = counts_at(offset - HALF, length + block_len)
    first_mean = window_sum(extended, length + block_len, ma_band, block_len).reshape(
        row_count, length + block_len
    )
    widened = jnp.where(inside[None, :], first_mean / wide_counts, 0.0)
    smooth_mean = (
        window_sum(widened, length, ma_band, block_len).reshape(row_count, length) / local_counts
    )
    detrended = dispersed - smooth_mean
    padding = jnp.zeros((row_count, HALF), jnp.float32)
    power_sum = lax.psum(jnp.sum(detrended * detrended, axis=1), "tm")
    row_spread_scale = jnp.sqrt(power_sum / total_len + eps_value)
    normed = detrended / row_spread_scale[:, None]
    colsum = lax.psum(jnp.sum(normed, axis=0), "dm")
    cleaned = normed - (colsum / (row_count * lax.axis_size("dm")))[None, :]
    head_cols = from_behind(cleaned[:, :HALF], "tm", -1)
    series = boxcar(
        jnp.concatenate([cleaned, head_cols, padding], axis=1), length, box_band, inverse, block_len
    )
    peak_values = lax.pmax(jnp.max(series, axis=2), "tm")
    return (series.astype(jnp.bfloat16), peak_values)


def solution(mesh):
    placed = (P("dm", "tm"), P())
    return jax.shard_map(
        body,
        mesh=mesh,
        in_specs=placed,
        out_specs=(P(None, "dm", "tm"), P(None, "dm")),
        check_vma=False,
    )
```

profile of v0, /device:TPU:0, one launch (start us, length us, event | category | flops | bytes accessed | tf_op | source)
XLA Modules:
  0.0 112.8 jit_solution(7534095986708861592)
XLA Ops:
  0.6 1.6 %copy.23 = f32[256,1024]{0,1:T(8,128)S(1)} copy(f32[256,1024]{1,0:T(8,128)} %param.2) | data formatting | bytes 2097152 | tf_op args[0]
  2.3 2.4 %collective-permute-start = (f32[256,256]{0,1:T(8,128)S(1)}, f32[256,256]{0,1:T(8,128)S(1)}, u32[]{:S(2)}, u32[]{:S(2)}) collective-permute-start(f32[256,256]{0,1:T(8,128)S(1)} %get-tuple-element.12), channel_id=1, source_target_pairs={{0,1},{1,2},{2,3},{3,4},{4,5},{5,6},{6,7},{8,9},{9,10},{10,11},{11... | collective-permute-start | bytes 786440 | tf_op jit(solution)/shard_map/ppermute | solution.py:19
  4.7 1.3 %collective-permute-start.1 = (f32[256,256]{0,1:T(8,128)S(1)}, f32[256,256]{0,1:T(8,128)S(1)}, u32[]{:S(2)}, u32[]{:S(2)}) collective-permute-start(f32[256,256]{0,1:T(8,128)S(1)} %get-tuple-element.13), channel_id=1, source_target_pairs={{1,0},{2,1},{3,2},{4,3},{5,4},{6,5},{7,6},{9,8},{10,9},{11,10},{12... | collective-permute-start | bytes 786440 | tf_op jit(solution)/shard_map/ppermute | solution.py:20
  6.1 4.0 %collective-permute-done.1 = f32[256,256]{0,1:T(8,128)S(1)} collective-permute-done((f32[256,256]{0,1:T(8,128)S(1)}, f32[256,256]{0,1:T(8,128)S(1)}, u32[]{:S(2)}, u32[]{:S(2)}) %collective-permute-start.1) | collective-permute-done | bytes 262176 | tf_op jit(solution)/shard_map/ppermute | solution.py:20
  10.3 1.3 %fusion.40 = (f32[256,5,256]{0,2,1:T(8,128)}, f32[256,5,256]{0,2,1:T(8,128)S(1)}) fusion(f32[256,6,256]{0,2,1:T(8,128)S(1)} %bitcast.22), kind=kLoop, calls=%fused_computation.58 | loop fusion | bytes 5242880 | tf_op jit(solution)/shard_map/slice | solution.py:44
  11.6 2.8 %copy.29 = f32[256,5,256]{2,0,1:T(8,128)} copy(f32[256,5,256]{0,2,1:T(8,128)} %get-tuple-element.6) | data formatting | bytes 2621440
  14.4 1.5 %copy.30 = f32[256,5,256]{2,0,1:T(8,128)} copy(f32[256,5,256]{0,2,1:T(8,128)S(1)} %get-tuple-element.7) | data formatting | bytes 2621440
  15.8 3.4 %divide_select_fusion = f32[256,5,256]{0,2,1:T(8,128)S(1)} fusion(f32[256,5,256]{2,0,1:T(8,128)} %copy.30, f32[256,5,256]{2,0,1:T(8,128)} %copy.29, f32[5,256]{1,0:T(8,128)S(1)} %add_convert_fusion, pred[5,256]{1,0:T(8,128)(4,1)S(1)} %fusion.31, s32[256]{0:T(256)S(1)} %get-tuple-element.15, s32[256]{0:T(256)S(1)} %get-tuple-element.14), kind=kOutput, calls=%fused_computation.20 | convolution fusion | flops 2014969856 | bytes 3940608 | tf_op jit(solution)/shard_map/rbs,sk->rbk/dot_general | solution.py:45
  19.4 1.3 %fusion.4 = f32[256,4,256]{0,2,1:T(8,128)S(1)} fusion(f32[256,4,256]{0,2,1:T(8,128)S(1)} %get-tuple-element.11, f32[256,4,256]{0,2,1:T(8,128)S(1)} %get-tuple-element.10, s32[256]{0:T(256)S(1)} %get-tuple-element.15, s32[256]{0:T(256)S(1)} %get-tuple-element.14), kind=kOutput, calls=%fused_computation.6 | convolution fusion | flops 1611530240 | bytes 3147776 | tf_op jit(solution)/shard_map/rbs,sk->rbk/dot_general | solution.py:45
  20.7 0.3 multiply_reduce_fusion.1
  21.0 16.6 %psum.14 = f32[256]{0:T(256)S(1)} all-reduce(f32[256]{0:T(256)S(1)} %get-tuple-element.4), channel_id=1, replica_groups=mesh['dm'=4,'tm'=8] {'tm'}, use_global_device_ids=true, to_apply=%region_1.2 | all-reduce | flops 256 | bytes 2048 | tf_op jit(solution)/shard_map/psum | solution.py:85
  37.8 12.0 %psum.15 = f32[1024]{0:T(1024)S(1)} all-reduce(f32[1024]{0:T(1024)S(1)} %fusion.22), channel_id=1, replica_groups=mesh['dm'=4,'tm'=8] {'dm'}, use_global_device_ids=true, to_apply=%region_3.4 | all-reduce | flops 1024 | bytes 8192 | tf_op jit(solution)/shard_map/psum | solution.py:88
  50.0 1.3 %collective-permute-start.2 = (f32[256,128]{0,1:T(8,128)S(1)}, f32[256,128]{0,1:T(8,128)S(1)}, u32[]{:S(2)}, u32[]{:S(2)}) collective-permute-start(f32[256,128]{0,1:T(8,128)S(1)} %slice.42), channel_id=1, source_target_pairs={{1,0},{2,1},{3,2},{4,3},{5,4},{6,5},{7,6},{9,8},{10,9},{11,10},{12... | collective-permute-start | bytes 393224 | tf_op jit(solution)/shard_map/ppermute | solution.py:28
  51.4 1.9 %collective-permute-done.2 = f32[256,128]{0,1:T(8,128)S(1)} collective-permute-done((f32[256,128]{0,1:T(8,128)S(1)}, f32[256,128]{0,1:T(8,128)S(1)}, u32[]{:S(2)}, u32[]{:S(2)}) %collective-permute-start.2) | collective-permute-done | bytes 131104 | tf_op jit(solution)/shard_map/ppermute | solution.py:28
  53.7 0.3 copy.31
  54.0 0.3 copy.32
  54.4 5.2 %fusion.8 = f32[256,4,1024]{2,0,1:T(8,128)} fusion(f32[256,4,256]{2,0,1:T(8,128)S(1)} %copy.32, f32[256,4,256]{2,0,1:T(8,128)S(1)} %copy.31, s32[1024]{0:T(1024)S(1)} %get-tuple-element.17, s32[1024]{0:T(1024)S(1)} %get-tuple-element.16), kind=kOutput, calls=%fused_computation.10 | convolution fusion | flops 6444548096 | bytes 6299648 | tf_op jit(solution)/shard_map/rbs,sk->rbk/dot_general | solution.py:45
  59.6 5.6 %reshape.95 = f32[256,4,4,256]{3,2,0,1:T(4,128)} reshape(f32[256,4,1024]{2,0,1:T(8,128)} %fusion.8) | data formatting | bytes 8388608 | tf_op jit(solution)/shard_map/reshape | solution.py:51
  65.2 3.2 %multiply_reduce_fusion = f32[4,256]{0,1:T(8,128)S(1)} fusion(f32[4]{0:T(128)S(1)} %convert_rsqrt_fusion, f32[256,4,4,256]{3,2,0,1:T(4,128)} %reshape.95), kind=kLoop, calls=%fused_computation | loop fusion | flops 2096128 | bytes 4198416 | tf_op jit(solution)/shard_map/reduce_max | solution.py:94
  68.4 26.9 %pmax.7 = f32[4,256]{0,1:T(8,128)S(1)} all-reduce(f32[4,256]{0,1:T(8,128)S(1)} %multiply_reduce_fusion), channel_id=1, replica_groups=mesh['dm'=4,'tm'=8] {'tm'}, use_global_device_ids=true, to_apply=%region_5.6 | all-reduce | flops 1024 | bytes 8192 | tf_op jit(solution)/shard_map/pmax | solution.py:94
  95.3 0.7 copy.27
  96.0 6.9 %copy.26 = f32[4,256,4,256]{3,2,1,0:T(4,128)} copy(f32[4,256,4,256]{3,0,1,2:T(4,128)} %bitcast.21) | data formatting | bytes 8388608 | tf_op jit(solution)/shard_map/transpose | solution.py:52
  102.9 5.8 %reshape.96 = f32[4,256,1024]{2,1,0:T(8,128)} reshape(f32[4,256,4,256]{3,2,1,0:T(4,128)} %copy.26) | data formatting | bytes 8388608 | tf_op jit(solution)/shard_map/reshape | solution.py:52
  108.7 4.1 %multiply_convert_fusion = bf16[4,256,1024]{2,1,0:T(8,128)(2,1)} fusion(f32[4,256,1024]{2,1,0:T(8,128)} %reshape.96, f32[4]{0:T(128)S(1)} %convert_rsqrt_fusion), kind=kLoop, calls=%fused_computation.1 | loop fusion | flops 2097152 | bytes 6291472 | tf_op jit(solution)/shard_map/convert_element_type | solution.py:95
  (23 shorter events, 1.3 us)
Async XLA Ops:
  0.6 5.4 %copy-start = (s32[4]{0:T(128)S(1)}, s32[4]{0:T(128)}, u32[]{:S(2)}) copy-start(s32[4]{0:T(128)} %param.3) | copy-start | bytes 52
  2.3 3.9 %collective-permute-start = (f32[256,256]{0,1:T(8,128)S(1)}, f32[256,256]{0,1:T(8,128)S(1)}, u32[]{:S(2)}, u32[]{:S(2)}) collective-permute-start(f32[256,256]{0,1:T(8,128)S(1)} %get-tuple-element.12), channel_id=1, source_target_pairs={{0,1},{1,2},{2,3},{3,4},{4,5},{5,6},{6,7},{8,9},{9,10},{10,11},{11... | collective-permute-start | bytes 786440 | tf_op jit(solution)/shard_map/ppermute | solution.py:19
  4.7 5.5 %collective-permute-start.1 = (f32[256,256]{0,1:T(8,128)S(1)}, f32[256,256]{0,1:T(8,128)S(1)}, u32[]{:S(2)}, u32[]{:S(2)}) collective-permute-start(f32[256,256]{0,1:T(8,128)S(1)} %get-tuple-element.13), channel_id=1, source_target_pairs={{1,0},{2,1},{3,2},{4,3},{5,4},{6,5},{7,6},{9,8},{10,9},{11,10},{12... | collective-permute-start | bytes 786440 | tf_op jit(solution)/shard_map/ppermute | solution.py:20
  50.0 3.2 %collective-permute-start.2 = (f32[256,128]{0,1:T(8,128)S(1)}, f32[256,128]{0,1:T(8,128)S(1)}, u32[]{:S(2)}, u32[]{:S(2)}) collective-permute-start(f32[256,128]{0,1:T(8,128)S(1)} %slice.42), channel_id=1, source_target_pairs={{1,0},{2,1},{3,2},{4,3},{5,4},{6,5},{7,6},{9,8},{10,9},{11,10},{12... | collective-permute-start | bytes 393224 | tf_op jit(solution)/shard_map/ppermute | solution.py:28
where the time goes:
time: 114 us; the launch traced here: 113 us
  blocking collectives  55.5 us (49%)
  local copies, waits for them, and re-layouts  27.2 us (24%)
  matrix products  9.89 us (9%)
  other arithmetic  8.4 us (7%)
  waiting for transfers between devices  5.97 us (5%)
  starting transfers between devices  5 us (4%)
    pmax x1, blocking collectives, body(): peak_values = lax.pmax(jnp.max(series, axis=2), 'tm')  26.9 us
    psum x1, blocking collectives, body(): power_sum = lax.psum(jnp.sum(detrended * detrended, axis=1), 'tm')  16.6 us
    psum x1, blocking collectives, body(): colsum = lax.psum(jnp.sum(normed, axis=0), 'dm')  12 us
    dot_general x3, matrix products, window_sum(): jnp.einsum('rbs,sk->rbk', paired, band_matrix, precision=lax.Precision.HI...  9.89 us
    unnamed x10, local copies, waits for them, and re-layouts  7.21 us
    transpose x1, local copies, waits for them, and re-layouts, boxcar(): jnp.transpose(moving, (2, 0, 1, 3))  6.85 us
    reshape x1, local copies, waits for them, and re-layouts, boxcar(): jnp.transpose(moving, (2, 0, 1, 3))  5.78 us
    reshape x1, local copies, waits for them, and re-layouts, boxcar(): moving.reshape(row_count, length // block_len, inverse.shape[0], block_len)  5.62 us
  transfers between devices with their start and end apart: 3, of which 2 were waited for; matrix products, arithmetic and copies ran while one was open for 0% of the time, Pallas kernels for 0%

commit v1 on v0

v1 whole, which is shorter than its diff:
```python
import functools

import jax
import jax.numpy as jnp
from jax import lax
from jax.experimental import pallas as pl
from jax.experimental.pallas import tpu as pltpu
from jax.sharding import PartitionSpec as P

HALF = 128
BLK = 2 * HALF
LANES = 128
ROWS_STEP = 64
PIECES = 3
EPS = 1e-06
MESH = pl.DeviceIdType.MESH
F32 = jnp.float32
BF16 = jnp.bfloat16


def pieces_of(value):
    out = []
    for _ in range(PIECES):
        term = value.astype(BF16)
        out.append(term)
        value = value - term.astype(F32)
    return out


def put_pieces(ref, start, value):
    for p, term in enumerate(pieces_of(value)):
        ref[p, :, start : start + value.shape[1]] = term


def window_dot(ref, start, reach, band):
    total = None
    for p in range(PIECES):
        part = jnp.dot(ref[p, :, start : start + reach], band, preferred_element_type=F32)
        total = part if total is None else total + part
    return total


def kernel(
    n_tm, n_dm, widths_ref, x_ref, snr_ref, peaks_ref,
    xe, xs, fms, det, ds, boxes, band, box_band, power, colsum, top, best,
    load_sem, halo_send, halo_recv, power_send, power_recv, col_send, col_recv, top_send, top_recv,
):
    rows, length = x_ref.shape
    nbox = widths_ref.shape[0]
    blocks = length // BLK
    total_len = n_tm * length
    me = lax.axis_index("tm")
    mine = lax.axis_index("dm")
    offset = me * length
    has_left, has_right = me > 0, me < n_tm - 1
    edge = BLK + length

    def load(k, start, size):
        return pltpu.make_async_copy(
            x_ref.at[:, pl.ds(start, size)], xe.at[:, pl.ds(BLK + start, size)], load_sem.at[k]
        )

    loads = [load(0, 0, BLK), load(1, length - BLK, BLK), load(2, BLK, length - 2 * BLK)]
    for one in loads:
        one.start()

    barrier = pltpu.get_barrier_semaphore()
    for d in range(1, n_tm):
        pl.semaphore_signal(barrier, inc=1, device_id={"tm": lax.rem(me + d, n_tm)}, device_id_type=MESH)
    for d in range(1, n_dm):
        pl.semaphore_signal(barrier, inc=1, device_id={"dm": lax.rem(mine + d, n_dm)}, device_id_type=MESH)

    rows_i = lax.broadcasted_iota(jnp.int32, (2 * BLK, BLK), 0)
    cols_i = lax.broadcasted_iota(jnp.int32, (2 * BLK, BLK), 1)
    band[...] = jnp.where((rows_i >= cols_i) & (rows_i <= cols_i + BLK), 1.0, 0.0).astype(BF16)
    rows_b = lax.broadcasted_iota(jnp.int32, (BLK + HALF, BLK), 0)
    cols_b = lax.broadcasted_iota(jnp.int32, (BLK + HALF, BLK), 1)
    lag = rows_b - cols_b
    for i in range(nbox):
        hit = (lag >= 0) & (lag < widths_ref[i])
        box_band[:, i * BLK : (i + 1) * BLK] = jnp.where(hit, 1.0, 0.0).astype(BF16)

    pl.semaphore_wait(barrier, n_tm - 1 + n_dm - 1)

    right = {"tm": lax.rem(me + 1, n_tm)}
    left = {"tm": lax.rem(me + n_tm - 1, n_tm)}

    def move(src, dst, k, target):
        return pltpu.make_async_remote_copy(
            src_ref=src, dst_ref=dst, send_sem=halo_send.at[k], recv_sem=halo_recv.at[k],
            device_id=target, device_id_type=MESH,
        )

    to_right = move(xe.at[:, pl.ds(length, BLK)], xe.at[:, pl.ds(0, BLK)], 0, right)
    to_left = move(xe.at[:, pl.ds(BLK, BLK)], xe.at[:, pl.ds(edge, BLK)], 1, left)
    head = move(det.at[:, pl.ds(0, HALF)], det.at[:, pl.ds(length, HALF)], 2, left)

    loads[1].wait()

    @pl.when(has_right)
    def _():
        to_right.start()

    loads[0].wait()

    @pl.when(has_left)
    def _():
        to_left.start()

    @pl.when(jnp.logical_not(has_left))
    def _():
        xe[:, 0:BLK] = jnp.zeros((rows, BLK), F32)

    @pl.when(jnp.logical_not(has_right))
    def _():
        xe[:, edge : edge + BLK] = jnp.zeros((rows, BLK), F32)
        det[:, length : length + HALF] = jnp.zeros((rows, HALF), F32)

    loads[2].wait()

    def inverse_counts(first):
        pos = offset + first + lax.broadcasted_iota(jnp.int32, (1, BLK), 1)
        counts = jnp.minimum(pos + HALF, total_len - 1) - jnp.maximum(pos - HALF, 0) + 1
        inside = (pos >= 0) & (pos < total_len)
        return jnp.where(inside, 1.0 / counts.astype(F32), 0.0)

    def first_mean(j):
        sums = window_dot(xs, j * BLK, 2 * BLK, band[...])
        put_pieces(fms, j * BLK, sums * inverse_counts(j * BLK - HALF))

    def detrend(j):
        sums = window_dot(fms, j * BLK, 2 * BLK, band[...])
        value = xe[:, (j + 1) * BLK : (j + 2) * BLK] - sums * inverse_counts(j * BLK)
        det[:, j * BLK : (j + 1) * BLK] = value
        put_pieces(ds, j * BLK, value)

    for j in range(1, blocks + 1):
        put_pieces(xs, j * BLK, xe[:, j * BLK : (j + 1) * BLK])
    for j in range(1, blocks):
        first_mean(j)
    for j in range(1, blocks - 1):
        detrend(j)

    @pl.when(has_left)
    def _():
        to_right.wait_recv()

    put_pieces(xs, 0, xe[:, 0:BLK])
    first_mean(0)
    detrend(0)

    @pl.when(has_left)
    def _():
        head.start()

    @pl.when(has_right)
    def _():
        to_left.wait_recv()

    put_pieces(xs, edge, xe[:, edge : edge + BLK])
    first_mean(blocks)
    detrend(blocks - 1)

    def exchange(slots, send, recv, axis, size, index):
        copies = []
        for d in range(1, size):
            copies.append(
                pltpu.make_async_remote_copy(
                    src_ref=slots.at[0], dst_ref=slots.at[d], send_sem=send.at[d], recv_sem=recv.at[d],
                    device_id={axis: lax.rem(index + d, size)}, device_id_type=MESH,
                )
            )
        for one in copies:
            one.start()
        return copies

    squares = jnp.zeros((rows, LANES), F32)
    for c in range(length // LANES):
        part = det[:, c * LANES : (c + 1) * LANES]
        squares = squares + part * part
    power[0] = jnp.sum(jnp.transpose(squares), axis=0, keepdims=True)
    power_copies = exchange(power, power_send, power_recv, "tm", n_tm, me)

    def boxcar(j):
        sums = window_dot(ds, j * BLK, BLK + HALF, box_band[...])
        for i in range(nbox):
            boxes[i, :, j * BLK : (j + 1) * BLK] = sums[:, i * BLK : (i + 1) * BLK]

    early = blocks // 2
    for j in range(early):
        boxcar(j)

    @pl.when(has_right)
    def _():
        head.wait_recv()

    put_pieces(ds, length, det[:, length : length + HALF])

    for one in power_copies:
        one.wait_recv()
    power_sum = power[0]
    for d in range(1, n_tm):
        power_sum = power_sum + power[d]
    scale = 1.0 / jnp.sqrt(power_sum / total_len + EPS)
    scale_rows = jnp.transpose(jnp.broadcast_to(scale, (LANES, rows)))
    for c in range(length // LANES + 1):
        part = det[:, c * LANES : (c + 1) * LANES] * scale_rows
        colsum[0, :, c * LANES : (c + 1) * LANES] = jnp.sum(part, axis=0, keepdims=True)
    col_copies = exchange(colsum, col_send, col_recv, "dm", n_dm, mine)

    for j in range(early, blocks):
        boxcar(j)

    for one in col_copies:
        one.wait_recv()
    common = colsum[0]
    for d in range(1, n_dm):
        common = common + colsum[d]
    common = common / (rows * n_dm)
    lines = [common[:, j * BLK : (j + 1) * BLK + HALF] for j in range(blocks)]
    lines = lines + [jnp.zeros((-blocks % 8, BLK + HALF), F32)] if blocks % 8 else lines
    stacked = jnp.concatenate(lines, axis=0)
    common_boxes = None
    for term in pieces_of(stacked):
        part = jnp.dot(term, box_band[...], preferred_element_type=F32)
        common_boxes = part if common_boxes is None else common_boxes + part

    for i in range(nbox):
        width = jnp.full((1, LANES), widths_ref[i], jnp.int32).astype(F32)
        inverse = 1.0 / jnp.sqrt(width)
        rows_of = []
        for c in range(length // LANES):
            j, part = divmod(c * LANES, BLK)
            first = i * BLK + part
            rows_of.append(common_boxes[j : j + 1, first : first + LANES] * inverse)
        best_tops = []
        for r in range(rows // ROWS_STEP):
            span = slice(r * ROWS_STEP, (r + 1) * ROWS_STEP)
            factor = scale_rows[span] * inverse
            peak = None
            for c in range(length // LANES):
                cols = slice(c * LANES, (c + 1) * LANES)
                series = boxes[i, span, cols] * factor - rows_of[c]
                snr_ref[i, span, cols] = series.astype(BF16)
                peak = series if peak is None else jnp.maximum(peak, series)
            best[span, :] = peak
        top[0, i : i + 1, :] = jnp.max(jnp.transpose(best[...]), axis=0, keepdims=True)

    top_copies = exchange(top, top_send, top_recv, "tm", n_tm, me)
    for one in top_copies:
        one.wait_recv()
    peaks = top[0]
    for d in range(1, n_tm):
        peaks = jnp.maximum(peaks, top[d])
    peaks_ref[...] = peaks

    for one in power_copies + col_copies + top_copies:
        one.wait_send()

    @pl.when(has_right)
    def _():
        to_right.wait_send()

    @pl.when(has_left)
    def _():
        to_left.wait_send()
        head.wait_send()


def body(n_tm, n_dm, dispersed, widths):
    rows, length = dispersed.shape
    nbox = widths.shape[0]
    sems = pltpu.SemaphoreType.DMA
    return pl.pallas_call(
        functools.partial(kernel, n_tm, n_dm),
        out_shape=(
            jax.ShapeDtypeStruct((nbox, rows, length), BF16),
            jax.ShapeDtypeStruct((nbox, rows), F32),
        ),
        in_specs=[pl.BlockSpec(memory_space=pltpu.SMEM), pl.BlockSpec(memory_space=pl.ANY)],
        out_specs=(pl.BlockSpec(memory_space=pltpu.VMEM), pl.BlockSpec(memory_space=pltpu.VMEM)),
        scratch_shapes=[
            pltpu.VMEM((rows, length + 2 * BLK), F32),
            pltpu.VMEM((PIECES, rows, length + 2 * BLK), BF16),
            pltpu.VMEM((PIECES, rows, length + BLK), BF16),
            pltpu.VMEM((rows, length + HALF), F32),
            pltpu.VMEM((PIECES, rows, length + HALF), BF16),
            pltpu.VMEM((nbox, rows, length), F32),
            pltpu.VMEM((2 * BLK, BLK), BF16),
            pltpu.VMEM((BLK + HALF, nbox * BLK), BF16),
            pltpu.VMEM((n_tm, 1, rows), F32),
            pltpu.VMEM((n_dm, 1, length + HALF), F32),
            pltpu.VMEM((n_tm, nbox, rows), F32),
            pltpu.VMEM((rows, LANES), F32),
            sems((3,)), sems((3,)), sems((3,)),
            sems((n_tm,)), sems((n_tm,)),
            sems((n_dm,)), sems((n_dm,)),
            sems((n_tm,)), sems((n_tm,)),
        ],
        compiler_params=pltpu.CompilerParams(
            collective_id=0, has_side_effects=True, vmem_limit_bytes=40 * 1024 * 1024
        ),
        name="detrend_filter",
    )(widths, dispersed)


def solution(mesh):
    return jax.shard_map(
        functools.partial(body, mesh.shape["tm"], mesh.shape["dm"]),
        mesh=mesh,
        in_specs=(P("dm", "tm"), P()),
        out_specs=(P(None, "dm", "tm"), P(None, "dm")),
        check_vma=False,
    )
```

time: 114 us -> 31.5 us (0.28)
  blocking collectives: 55.5 us -> 0 us
  Pallas kernels: 0 us -> 26.9 us
  local copies, waits for them, and re-layouts: 27.2 us -> 3.79 us
  matrix products: 9.89 us -> 0 us
  other arithmetic: 8.4 us -> 0 us
  waiting for transfers between devices: 5.97 us -> 0 us
  starting transfers between devices: 5 us -> 0 us
    psum x2 -> x0, blocking collectives: 28.6 us -> none  [the longest x1 16.6 us: body(): power_sum = lax.psum(jnp.sum(detrended * detrended, axis=1), 'tm')]
    pmax x1 -> x0, blocking collectives: 26.9 us -> none  [body(): peak_values = lax.pmax(jnp.max(series, axis=2), 'tm')]
    pallas_call x0 -> x1, Pallas kernels: none -> 26.9 us  [body(): pl.pallas_call(functools.partial(kernel, n_tm, n_dm), out_shape=(jax.Shap...]
    reshape x2 -> x0, local copies, waits for them, and re-layouts: 11.4 us -> none  [the longest x1 5.78 us: boxcar(): jnp.transpose(moving, (2, 0, 1, 3))]
    dot_general x3 -> x0, matrix products: 9.89 us -> none  [window_sum(): jnp.einsum('rbs,sk->rbk', paired, band_matrix, precision=lax.Precision.HI...]
    transpose x1 -> x0, local copies, waits for them, and re-layouts: 6.85 us -> none  [boxcar(): jnp.transpose(moving, (2, 0, 1, 3))]
    ppermute x3 -> x0, waiting for transfers between devices: 5.97 us -> none  [the longest x1 4.03 us: with_halo(): after = lax.ppermute(leading, axis, down)]
    ppermute x3 -> x0, starting transfers between devices: 5 us -> none  [the longest x1 2.41 us: with_halo(): before = lax.ppermute(last, axis, up)]
  transfers between devices with their start and end apart: 3 -> 0, of which waited for: 2 -> 0; matrix products, arithmetic and copies ran while one was open for 0% -> 0% of each run, Pallas kernels for 0% -> 0%
where the time goes in v1:
time: 31.5 us; the launch traced here: 31.3 us
  Pallas kernels  26.9 us (85%)
  local copies, waits for them, and re-layouts  3.79 us (12%)
  between operations  0.65 us (2%)
    pallas_call x1, Pallas kernels, body(): pl.pallas_call(functools.partial(kernel, n_tm, n_dm), out_shape=(jax.Shap...  26.9 us
    unnamed x6, local copies, waits for them, and re-layouts  3.79 us

profile of v1, /device:TPU:0, one launch (start us, length us, event | category | flops | bytes accessed | tf_op | source)
XLA Modules:
  0.0 31.3 jit_solution(7817087923895281873)
XLA Ops:
  0.6 0.0 copy-start
  0.6 1.2 %copy-done = f32[256,1024]{1,0:T(8,128)S(1)} copy-done((f32[256,1024]{1,0:T(8,128)S(1)}, f32[256,1024]{1,0:T(8,128)}, u32[]{:S(2)}) %copy-start) | copy-done | bytes 1048600
  1.9 0.0 copy-start.1
  1.9 0.7 %copy-done.1 = s32[4]{0:T(128)S(1)} copy-done((s32[4]{0:T(128)S(1)}, s32[4]{0:T(128)}, u32[]{:S(2)}) %copy-start.1) | copy-done | bytes 40
  2.5 26.9 %detrend_filter.1 = (bf16[4,256,1024]{2,1,0:T(8,128)(2,1)S(1)}, f32[4,256]{1,0:T(4,128)S(1)}) custom-call(s32[4]{0:T(128)S(1)} %copy-done.1, f32[256,1024]{1,0:T(8,128)S(1)} %copy-done), custom_call_target="tpu_custom_call" | custom-call | tf_op jit(solution)/shard_map/detrend_filter/pallas_call | solution.py:274
  29.4 1.3 %copy.6 = bf16[4,256,1024]{2,1,0:T(8,128)(2,1)} copy(bf16[4,256,1024]{2,1,0:T(8,128)(2,1)S(1)} %get-tuple-element.4) | data formatting | bytes 4194304
  30.7 0.6 %copy.7 = f32[4,256]{1,0:T(4,128)} copy(f32[4,256]{1,0:T(4,128)S(1)} %get-tuple-element.5) | data formatting | bytes 8192
Async XLA Ops:
  0.6 1.2 %copy-start = (f32[256,1024]{1,0:T(8,128)S(1)}, f32[256,1024]{1,0:T(8,128)}, u32[]{:S(2)}) copy-start(f32[256,1024]{1,0:T(8,128)} %x_ref.1) | copy-start | bytes 3145732
  1.9 0.7 %copy-start.1 = (s32[4]{0:T(128)S(1)}, s32[4]{0:T(128)}, u32[]{:S(2)}) copy-start(s32[4]{0:T(128)} %widths_ref.1) | copy-start | bytes 52

commit v2 on v1

--- a/solution.py
+++ b/solution.py
@@ -41,12 +41,12 @@
 
 
 def kernel(
-    n_tm, n_dm, widths_ref, x_ref, snr_ref, peaks_ref,
-    xe, xs, fms, det, ds, boxes, band, box_band, power, colsum, top, best,
-    load_sem, halo_send, halo_recv, power_send, power_recv, col_send, col_recv, top_send, top_recv,
+    n_tm, n_dm, widths_hbm, x_ref, snr_ref, peaks_ref,
+    widths_ref, xe, xs, fms, det, ds, boxes, band, box_band, power, colsum, top, best,
+    width_sem, load_sem, halo_send, halo_recv, power_send, power_recv, col_send, col_recv, top_send, top_recv,
 ):
     rows, length = x_ref.shape
-    nbox = widths_ref.shape[0]
+    nbox = widths_hbm.shape[0]
     blocks = length // BLK
     total_len = n_tm * length
     me = lax.axis_index("tm")
@@ -61,6 +61,8 @@
         )
 
     loads = [load(0, 0, BLK), load(1, length - BLK, BLK), load(2, BLK, length - 2 * BLK)]
+    width_load = pltpu.make_async_copy(widths_hbm, widths_ref, width_sem)
+    width_load.start()
     for one in loads:
         one.start()
 
@@ -73,6 +75,7 @@
     rows_i = lax.broadcasted_iota(jnp.int32, (2 * BLK, BLK), 0)
     cols_i = lax.broadcasted_iota(jnp.int32, (2 * BLK, BLK), 1)
     band[...] = jnp.where((rows_i >= cols_i) & (rows_i <= cols_i + BLK), 1.0, 0.0).astype(BF16)
+    width_load.wait()
     rows_b = lax.broadcasted_iota(jnp.int32, (BLK + HALF, BLK), 0)
     cols_b = lax.broadcasted_iota(jnp.int32, (BLK + HALF, BLK), 1)
     lag = rows_b - cols_b
@@ -225,28 +228,36 @@
         part = jnp.dot(term, box_band[...], preferred_element_type=F32)
         common_boxes = part if common_boxes is None else common_boxes + part
 
+    def each_series(use):
+        for i in range(nbox):
+            width = jnp.full((1, LANES), widths_ref[i], jnp.int32).astype(F32)
+            inverse = 1.0 / jnp.sqrt(width)
+            shifts = []
+            for c in range(length // LANES):
+                j, part = divmod(c * LANES, BLK)
+                first = i * BLK + part
+                shifts.append(common_boxes[j : j + 1, first : first + LANES] * inverse)
+            for r in range(rows // ROWS_STEP):
+                span = slice(r * ROWS_STEP, (r + 1) * ROWS_STEP)
+                factor = scale_rows[span] * inverse
+                use(i, span, [
+                    boxes[i, span, c * LANES : (c + 1) * LANES] * factor - shifts[c]
+                    for c in range(length // LANES)
+                ])
+
+    def take_peak(i, span, parts):
+        best[i, span, :] = functools.reduce(jnp.maximum, parts)
+
+    def take_snr(i, span, parts):
+        for c, series in enumerate(parts):
+            snr_ref[i, span, c * LANES : (c + 1) * LANES] = series.astype(BF16)
+
+    each_series(take_peak)
     for i in range(nbox):
-        width = jnp.full((1, LANES), widths_ref[i], jnp.int32).astype(F32)
-        inverse = 1.0 / jnp.sqrt(width)
-        rows_of = []
-        for c in range(length // LANES):
-            j, part = divmod(c * LANES, BLK)
-            first = i * BLK + part
-            rows_of.append(common_boxes[j : j + 1, first : first + LANES] * inverse)
-        best_tops = []
-        for r in range(rows // ROWS_STEP):
-            span = slice(r * ROWS_STEP, (r + 1) * ROWS_STEP)
-            factor = scale_rows[span] * inverse
-            peak = None
-            for c in range(length // LANES):
-                cols = slice(c * LANES, (c + 1) * LANES)
-                series = boxes[i, span, cols] * factor - rows_of[c]
-                snr_ref[i, span, cols] = series.astype(BF16)
-                peak = series if peak is None else jnp.maximum(peak, series)
-            best[span, :] = peak
-        top[0, i : i + 1, :] = jnp.max(jnp.transpose(best[...]), axis=0, keepdims=True)
+        top[0, i : i + 1, :] = jnp.max(jnp.transpose(best[i]), axis=0, keepdims=True)
 
     top_copies = exchange(top, top_send, top_recv, "tm", n_tm, me)
+    each_series(take_snr)
     for one in top_copies:
         one.wait_recv()
     peaks = top[0]
@@ -267,19 +278,30 @@
         head.wait_send()
 
 
+def hand_out(snr_ref, peaks_ref, snr_out, peaks_out, sem):
+    nbox = snr_ref.shape[0]
+    copies = [pltpu.make_async_copy(snr_ref.at[i], snr_out.at[i], sem.at[i]) for i in range(nbox)]
+    copies.append(pltpu.make_async_copy(peaks_ref, peaks_out, sem.at[nbox]))
+    for one in copies:
+        one.start()
+    for one in copies:
+        one.wait()
+
+
 def body(n_tm, n_dm, dispersed, widths):
     rows, length = dispersed.shape
     nbox = widths.shape[0]
     sems = pltpu.SemaphoreType.DMA
-    return pl.pallas_call(
+    snr, peaks = pl.pallas_call(
         functools.partial(kernel, n_tm, n_dm),
         out_shape=(
             jax.ShapeDtypeStruct((nbox, rows, length), BF16),
             jax.ShapeDtypeStruct((nbox, rows), F32),
         ),
-        in_specs=[pl.BlockSpec(memory_space=pltpu.SMEM), pl.BlockSpec(memory_space=pl.ANY)],
+        in_specs=[pl.BlockSpec(memory_space=pltpu.HBM)] * 2,
         out_specs=(pl.BlockSpec(memory_space=pltpu.VMEM), pl.BlockSpec(memory_space=pltpu.VMEM)),
         scratch_shapes=[
+            pltpu.SMEM((nbox,), jnp.int32),
             pltpu.VMEM((rows, length + 2 * BLK), F32),
             pltpu.VMEM((PIECES, rows, length + 2 * BLK), BF16),
             pltpu.VMEM((PIECES, rows, length + BLK), BF16),
@@ -291,8 +313,8 @@
             pltpu.VMEM((n_tm, 1, rows), F32),
             pltpu.VMEM((n_dm, 1, length + HALF), F32),
             pltpu.VMEM((n_tm, nbox, rows), F32),
-            pltpu.VMEM((rows, LANES), F32),
-            sems((3,)), sems((3,)), sems((3,)),
+            pltpu.VMEM((nbox, rows, LANES), F32),
+            sems, sems((3,)), sems((3,)), sems((3,)),
             sems((n_tm,)), sems((n_tm,)),
             sems((n_dm,)), sems((n_dm,)),
             sems((n_tm,)), sems((n_tm,)),
@@ -301,7 +323,22 @@
             collective_id=0, has_side_effects=True, vmem_limit_bytes=40 * 1024 * 1024
         ),
         name="detrend_filter",
-    )(widths, dispersed)
+    )(
+        pltpu.with_memory_space_constraint(widths, pltpu.HBM),
+        pltpu.with_memory_space_constraint(dispersed, pltpu.HBM),
+    )
+    return pl.pallas_call(
+        hand_out,
+        out_shape=(
+            jax.ShapeDtypeStruct(snr.shape, BF16),
+            jax.ShapeDtypeStruct(peaks.shape, F32),
+        ),
+        in_specs=[pl.BlockSpec(memory_space=pltpu.VMEM)] * 2,
+        out_specs=(pl.BlockSpec(memory_space=pltpu.HBM), pl.BlockSpec(memory_space=pltpu.HBM)),
+        scratch_shapes=[sems((nbox + 1,))],
+        compiler_params=pltpu.CompilerParams(vmem_limit_bytes=1024 * 1024),
+        name="hand_out",
+    )(snr, peaks)
 
 
 def solution(mesh):

time: 31.5 us -> 28.2 us (0.90)
  local copies, waits for them, and re-layouts: 3.79 us -> 0 us
  Pallas kernels: 26.9 us -> 27.5 us
    unnamed x6 -> x0, local copies, waits for them, and re-layouts: 3.79 us -> none
    pallas_call x0 -> x1, Pallas kernels: none -> 1.36 us  [body(): pl.pallas_call(hand_out, out_shape=(jax.ShapeDtypeStruct(snr.shape, BF16)...]
    pallas_call x1, Pallas kernels: 26.9 us -> 26.1 us  [body(): pl.pallas_call(functools.partial(kernel, n_tm, n_dm), out_shape=(jax.Shap...]
where the time goes in v2:
time: 28.2 us; the launch traced here: 28.1 us
  Pallas kernels  27.5 us (98%)
  between operations  0.64 us (2%)
    pallas_call x1, Pallas kernels, body(): pl.pallas_call(functools.partial(kernel, n_tm, n_dm), out_shape=(jax.Shap...  26.1 us
    pallas_call x1, Pallas kernels, body(): pl.pallas_call(hand_out, out_shape=(jax.ShapeDtypeStruct(snr.shape, BF16)...  1.36 us

profile of v2, /device:TPU:0, one launch (start us, length us, event | category | flops | bytes accessed | tf_op | source)
XLA Modules:
  0.0 28.1 jit_solution(6348270260905799581)
XLA Ops:
  0.6 26.1 %detrend_filter.1 = (bf16[4,256,1024]{2,1,0:T(8,128)(2,1)S(1)}, f32[4,256]{1,0:T(4,128)S(1)}) custom-call(s32[4]{0:T(128)} %widths_hbm.1, f32[256,1024]{1,0:T(8,128)} %x_ref.1), custom_call_target="tpu_custom_call" | custom-call | tf_op jit(solution)/shard_map/detrend_filter/pallas_call | solution.py:295
  26.7 1.4 %hand_out.1 = (bf16[4,256,1024]{2,1,0:T(8,128)(2,1)}, f32[4,256]{1,0:T(4,128)}) custom-call(bf16[4,256,1024]{2,1,0:T(8,128)(2,1)S(1)} %get-tuple-element.4.snr_ref, f32[4,256]{1,0:T(4,128)S(1)} %get-tuple-element.5.peaks_ref), custom_call_target="tpu_custom_call" | custom-call | tf_op jit(solution)/shard_map/hand_out/pallas_call | solution.py:330

commit v3 on v2

--- a/solution.py
+++ b/solution.py
@@ -42,7 +42,7 @@
 
 def kernel(
     n_tm, n_dm, widths_hbm, x_ref, snr_ref, peaks_ref,
-    widths_ref, xe, xs, fms, det, ds, boxes, band, box_band, power, colsum, top, best,
+    widths_ref, ahead, squares, xe, xs, fms, det, ds, boxes, band, box_band, power, colsum, top, best,
     width_sem, load_sem, halo_send, halo_recv, power_send, power_recv, col_send, col_recv, top_send, top_recv,
 ):
     rows, length = x_ref.shape
@@ -96,7 +96,7 @@
 
     to_right = move(xe.at[:, pl.ds(length, BLK)], xe.at[:, pl.ds(0, BLK)], 0, right)
     to_left = move(xe.at[:, pl.ds(BLK, BLK)], xe.at[:, pl.ds(edge, BLK)], 1, left)
-    head = move(det.at[:, pl.ds(0, HALF)], det.at[:, pl.ds(length, HALF)], 2, left)
+    beyond = move(xe.at[:, pl.ds(2 * BLK, HALF)], xe.at[:, pl.ds(edge + BLK, HALF)], 2, left)
 
     loads[1].wait()
 
@@ -116,53 +116,74 @@
 
     @pl.when(jnp.logical_not(has_right))
     def _():
-        xe[:, edge : edge + BLK] = jnp.zeros((rows, BLK), F32)
-        det[:, length : length + HALF] = jnp.zeros((rows, HALF), F32)
+        xe[:, edge : edge + BLK + HALF] = jnp.zeros((rows, BLK + HALF), F32)
 
     loads[2].wait()
 
-    def inverse_counts(first):
-        pos = offset + first + lax.broadcasted_iota(jnp.int32, (1, BLK), 1)
+    @pl.when(has_left)
+    def _():
+        beyond.start()
+
+    def inverse_counts(first, size):
+        pos = offset + first + lax.broadcasted_iota(jnp.int32, (1, size), 1)
         counts = jnp.minimum(pos + HALF, total_len - 1) - jnp.maximum(pos - HALF, 0) + 1
         inside = (pos >= 0) & (pos < total_len)
         return jnp.where(inside, 1.0 / counts.astype(F32), 0.0)
 
-    def first_mean(j):
-        sums = window_dot(xs, j * BLK, 2 * BLK, band[...])
-        put_pieces(fms, j * BLK, sums * inverse_counts(j * BLK - HALF))
-
-    def detrend(j):
-        sums = window_dot(fms, j * BLK, 2 * BLK, band[...])
-        value = xe[:, (j + 1) * BLK : (j + 2) * BLK] - sums * inverse_counts(j * BLK)
-        det[:, j * BLK : (j + 1) * BLK] = value
-        put_pieces(ds, j * BLK, value)
-
+    def put_mean(start, sums):
+        put_pieces(fms, start, sums * inverse_counts(start - HALF, sums.shape[1]))
+
+    def put_detrended(start, sums):
+        size = sums.shape[1]
+        value = xe[:, BLK + start : BLK + start + size] - sums * inverse_counts(start, size)
+        det[:, start : start + size] = value
+        put_pieces(ds, start, value)
+
+    def square_sum(first, last):
+        total = None
+        for c in range(first, last, LANES):
+            part = det[:, c : c + LANES]
+            total = part * part if total is None else total + part * part
+        return total
+
+    def full(ref, start):
+        return window_dot(ref, start, 2 * BLK, band[...])
+
+    def upper(ref, start):
+        return window_dot(ref, start, BLK, band[0:BLK, :])
+
+    def lower(ref, start):
+        return window_dot(ref, start, BLK, band[BLK:, :])
+
+    last = length - BLK
     for j in range(1, blocks + 1):
         put_pieces(xs, j * BLK, xe[:, j * BLK : (j + 1) * BLK])
     for j in range(1, blocks):
-        first_mean(j)
+        put_mean(j * BLK, full(xs, j * BLK))
     for j in range(1, blocks - 1):
-        detrend(j)
+        put_detrended(j * BLK, full(fms, j * BLK))
+    ahead[0] = lower(xs, BLK)
+    ahead[1] = upper(xs, length)
+    ahead[2] = lower(fms, BLK)
+    ahead[3] = upper(fms, last)
+    squares[...] = square_sum(BLK, last)
 
     @pl.when(has_left)
     def _():
         to_right.wait_recv()
 
     put_pieces(xs, 0, xe[:, 0:BLK])
-    first_mean(0)
-    detrend(0)
-
-    @pl.when(has_left)
-    def _():
-        head.start()
+    put_mean(0, ahead[0] + upper(xs, 0))
+    put_detrended(0, ahead[2] + upper(fms, 0))
+    squares[...] += square_sum(0, BLK)
 
     @pl.when(has_right)
     def _():
         to_left.wait_recv()
 
     put_pieces(xs, edge, xe[:, edge : edge + BLK])
-    first_mean(blocks)
-    detrend(blocks - 1)
+    put_mean(length, ahead[1] + lower(xs, edge))
+    put_detrended(last, ahead[3] + lower(fms, length))
 
     def exchange(slots, send, recv, axis, size, index):
         copies = []
@@ -177,11 +198,8 @@
             one.start()
         return copies
 
-    squares = jnp.zeros((rows, LANES), F32)
-    for c in range(length // LANES):
-        part = det[:, c * LANES : (c + 1) * LANES]
-        squares = squares + part * part
-    power[0] = jnp.sum(jnp.transpose(squares), axis=0, keepdims=True)
+    all_squares = squares[...] + square_sum(last, length)
+    power[0] = jnp.sum(jnp.transpose(all_squares), axis=0, keepdims=True)
     power_copies = exchange(power, power_send, power_recv, "tm", n_tm, me)
 
     def boxcar(j):
@@ -195,9 +213,12 @@
 
     @pl.when(has_right)
     def _():
-        head.wait_recv()
-
-    put_pieces(ds, length, det[:, length : length + HALF])
+        beyond.wait_recv()
+
+    short = band[0 : BLK + HALF, 0:HALF]
+    put_pieces(xs, edge + BLK, xe[:, edge + BLK : edge + BLK + HALF])
+    put_mean(edge, window_dot(xs, edge, BLK + HALF, short))
+    put_detrended(length, window_dot(fms, length, BLK + HALF, short))
 
     for one in power_copies:
         one.wait_recv()
@@ -275,7 +296,7 @@
     @pl.when(has_left)
     def _():
         to_left.wait_send()
-        head.wait_send()
+        beyond.wait_send()
 
 
 def hand_out(snr_ref, peaks_ref, snr_out, peaks_out, sem):
@@ -302,9 +323,11 @@
         out_specs=(pl.BlockSpec(memory_space=pltpu.VMEM), pl.BlockSpec(memory_space=pltpu.VMEM)),
         scratch_shapes=[
             pltpu.SMEM((nbox,), jnp.int32),
-            pltpu.VMEM((rows, length + 2 * BLK), F32),
-            pltpu.VMEM((PIECES, rows, length + 2 * BLK), BF16),
-            pltpu.VMEM((PIECES, rows, length + BLK), BF16),
+            pltpu.VMEM((4, rows, BLK), F32),
+            pltpu.VMEM((rows, LANES), F32),
+            pltpu.VMEM((rows, length + 2 * BLK + HALF), F32),
+            pltpu.VMEM((PIECES, rows, length + 2 * BLK + HALF), BF16),
+            pltpu.VMEM((PIECES, rows, length + BLK + HALF), BF16),
             pltpu.VMEM((rows, length + HALF), F32),
             pltpu.VMEM((PIECES, rows, length + HALF), BF16),
             pltpu.VMEM((nbox, rows, length), F32),

time: 28.2 us -> 27 us (0.957)
  Pallas kernels: 27.5 us -> 26.2 us
    pallas_call x1, Pallas kernels: 26.1 us -> 24.8 us  [body(): pl.pallas_call(functools.partial(kernel, n_tm, n_dm), out_shape=(jax.Shap...]
where the time goes in v3:
time: 27 us; the launch traced here: 26.8 us
  Pallas kernels  26.2 us (97%)
  between operations  0.64 us (2%)
    pallas_call x1, Pallas kernels, body(): pl.pallas_call(functools.partial(kernel, n_tm, n_dm), out_shape=(jax.Shap...  24.8 us
    pallas_call x1, Pallas kernels, body(): pl.pallas_call(hand_out, out_shape=(jax.ShapeDtypeStruct(snr.shape, BF16)...  1.36 us

profile of v3, /device:TPU:0, one launch (start us, length us, event | category | flops | bytes accessed | tf_op | source)
XLA Modules:
  0.0 26.8 jit_solution(17045732895968195725)
XLA Ops:
  0.6 24.8 %detrend_filter.1 = (bf16[4,256,1024]{2,1,0:T(8,128)(2,1)S(1)}, f32[4,256]{1,0:T(4,128)S(1)}) custom-call(s32[4]{0:T(128)} %widths_hbm.1, f32[256,1024]{1,0:T(8,128)} %x_ref.1), custom_call_target="tpu_custom_call" | custom-call | tf_op jit(solution)/shard_map/detrend_filter/pallas_call | solution.py:316
  25.5 1.4 %hand_out.1 = (bf16[4,256,1024]{2,1,0:T(8,128)(2,1)}, f32[4,256]{1,0:T(4,128)}) custom-call(bf16[4,256,1024]{2,1,0:T(8,128)(2,1)S(1)} %get-tuple-element.4.snr_ref, f32[4,256]{1,0:T(4,128)S(1)} %get-tuple-element.5.peaks_ref), custom_call_target="tpu_custom_call" | custom-call | tf_op jit(solution)/shard_map/hand_out/pallas_call | solution.py:353

commit v4 on v3

--- a/solution.py
+++ b/solution.py
@@ -27,15 +27,15 @@
     return out
 
 
-def put_pieces(ref, start, value):
+def put_pieces(ref, start, value, span=slice(None)):
     for p, term in enumerate(pieces_of(value)):
-        ref[p, :, start : start + value.shape[1]] = term
-
-
-def window_dot(ref, start, reach, band):
+        ref[p, span, start : start + value.shape[1]] = term
+
+
+def window_dot(ref, start, reach, band, span=slice(None)):
     total = None
     for p in range(PIECES):
-        part = jnp.dot(ref[p, :, start : start + reach], band, preferred_element_type=F32)
+        part = jnp.dot(ref[p, span, start : start + reach], band, preferred_element_type=F32)
         total = part if total is None else total + part
     return total
 
@@ -94,21 +94,34 @@
             device_id=target, device_id_type=MESH,
         )
 
-    to_right = move(xe.at[:, pl.ds(length, BLK)], xe.at[:, pl.ds(0, BLK)], 0, right)
-    to_left = move(xe.at[:, pl.ds(BLK, BLK)], xe.at[:, pl.ds(edge, BLK)], 1, left)
-    beyond = move(xe.at[:, pl.ds(2 * BLK, HALF)], xe.at[:, pl.ds(edge + BLK, HALF)], 2, left)
+    half = rows // 2
+    spans = [slice(0, half), slice(half, rows)]
+
+    def right_halo(h):
+        span = pl.ds(h * half, half)
+        return move(xe.at[span, pl.ds(length, BLK)], xe.at[span, pl.ds(0, BLK)], 2 * h, right)
+
+    def left_halo(h):
+        span = pl.ds(h * half, half)
+        return move(xe.at[span, pl.ds(BLK, BLK)], xe.at[span, pl.ds(edge, BLK)], 2 * h + 1, left)
+
+    to_right = [right_halo(0), right_halo(1)]
+    to_left = [left_halo(0), left_halo(1)]
+    beyond = move(xe.at[:, pl.ds(2 * BLK, HALF)], xe.at[:, pl.ds(edge + BLK, HALF)], 4, left)
 
     loads[1].wait()
 
     @pl.when(has_right)
     def _():
-        to_right.start()
+        for one in to_right:
+            one.start()
 
     loads[0].wait()
 
     @pl.when(has_left)
     def _():
-        to_left.start()
+        for one in to_left:
+            one.start()
 
     @pl.when(jnp.logical_not(has_left))
     def _():
@@ -130,14 +143,14 @@
         inside = (pos >= 0) & (pos < total_len)
         return jnp.where(inside, 1.0 / counts.astype(F32), 0.0)
 
-    def put_mean(start, sums):
-        put_pieces(fms, start, sums * inverse_counts(start - HALF, sums.shape[1]))
-
-    def put_detrended(start, sums):
+    def put_mean(start, sums, span=slice(None)):
+        put_pieces(fms, start, sums * inverse_counts(start - HALF, sums.shape[1]), span)
+
+    def put_detrended(start, sums, span=slice(None)):
         size = sums.shape[1]
-        value = xe[:, BLK + start : BLK + start + size] - sums * inverse_counts(start, size)
-        det[:, start : start + size] = value
-        put_pieces(ds, start, value)
+        value = xe[span, BLK + start : BLK + start + size] - sums * inverse_counts(start, size)
+        det[span, start : start + size] = value
+        put_pieces(ds, start, value, span)
 
     def square_sum(first, last):
         total = None
@@ -149,11 +162,11 @@
     def full(ref, start):
         return window_dot(ref, start, 2 * BLK, band[...])
 
-    def upper(ref, start):
-        return window_dot(ref, start, BLK, band[0:BLK, :])
-
-    def lower(ref, start):
-        return window_dot(ref, start, BLK, band[BLK:, :])
+    def upper(ref, start, span=slice(None)):
+        return window_dot(ref, start, BLK, band[0:BLK, :], span)
+
+    def lower(ref, start, span=slice(None)):
+        return window_dot(ref, start, BLK, band[BLK:, :], span)
 
     last = length - BLK
     for j in range(1, blocks + 1):
@@ -168,22 +181,30 @@
     ahead[3] = upper(fms, last)
     squares[...] = square_sum(BLK, last)
 
-    @pl.when(has_left)
-    def _():
-        to_right.wait_recv()
-
-    put_pieces(xs, 0, xe[:, 0:BLK])
-    put_mean(0, ahead[0] + upper(xs, 0))
-    put_detrended(0, ahead[2] + upper(fms, 0))
+    def left_edge(span):
+        put_pieces(xs, 0, xe[span, 0:BLK], span)
+        put_mean(0, ahead[0, span] + upper(xs, 0, span), span)
+        put_detrended(0, ahead[2, span] + upper(fms, 0, span), span)
+
+    def right_edge(span):
+        put_pieces(xs, edge, xe[span, edge : edge + BLK], span)
+        put_mean(length, ahead[1, span] + lower(xs, edge, span), span)
+        put_detrended(last, ahead[3, span] + lower(fms, length, span), span)
+
+    for h, span in enumerate(spans):
+        @pl.when(has_left)
+        def _(one=to_right[h]):
+            one.wait_recv()
+
+        left_edge(span)
+
+        @pl.when(has_right)
+        def _(one=to_left[h]):
+            one.wait_recv()
+
+        right_edge(span)
+
     squares[...] += square_sum(0, BLK)
-
-    @pl.when(has_right)
-    def _():
-        to_left.wait_recv()
-
-    put_pieces(xs, edge, xe[:, edge : edge + BLK])
-    put_mean(length, ahead[1] + lower(xs, edge))
-    put_detrended(last, ahead[3] + lower(fms, length))
 
     def exchange(slots, send, recv, axis, size, index):
         copies = []
@@ -244,10 +265,12 @@
     lines = [common[:, j * BLK : (j + 1) * BLK + HALF] for j in range(blocks)]
     lines = lines + [jnp.zeros((-blocks % 8, BLK + HALF), F32)] if blocks % 8 else lines
     stacked = jnp.concatenate(lines, axis=0)
-    common_boxes = None
-    for term in pieces_of(stacked):
-        part = jnp.dot(term, box_band[...], preferred_element_type=F32)
-        common_boxes = part if common_boxes is None else common_boxes + part
+    height = stacked.shape[0]
+    terms = jnp.concatenate([term.astype(F32) for term in pieces_of(stacked)], axis=0).astype(BF16)
+    parts = jnp.dot(terms, box_band[...], preferred_element_type=F32)
+    common_boxes = parts[0:height]
+    for p in range(1, PIECES):
+        common_boxes = common_boxes + parts[p * height : (p + 1) * height]
 
     def each_series(use):
         for i in range(nbox):
@@ -291,11 +314,13 @@
 
     @pl.when(has_right)
     def _():
-        to_right.wait_send()
+        for one in to_right:
+            one.wait_send()
 
     @pl.when(has_left)
     def _():
-        to_left.wait_send()
+        for one in to_left:
+            one.wait_send()
         beyond.wait_send()
 
 
@@ -337,7 +362,7 @@
             pltpu.VMEM((n_dm, 1, length + HALF), F32),
             pltpu.VMEM((n_tm, nbox, rows), F32),
             pltpu.VMEM((nbox, rows, LANES), F32),
-            sems, sems((3,)), sems((3,)), sems((3,)),
+            sems, sems((3,)), sems((5,)), sems((5,)),
             sems((n_tm,)), sems((n_tm,)),
             sems((n_dm,)), sems((n_dm,)),
             sems((n_tm,)), sems((n_tm,)),

time: 27 us -> 26.4 us (0.978)
  Pallas kernels: 26.2 us -> 25.7 us
    pallas_call x1, Pallas kernels: 24.8 us -> 24.3 us  [body(): pl.pallas_call(functools.partial(kernel, n_tm, n_dm), out_shape=(jax.Shap...]
where the time goes in v4:
time: 26.4 us; the launch traced here: 26.3 us
  Pallas kernels  25.7 us (97%)
  between operations  0.64 us (2%)
    pallas_call x1, Pallas kernels, body(): pl.pallas_call(functools.partial(kernel, n_tm, n_dm), out_shape=(jax.Shap...  24.3 us
    pallas_call x1, Pallas kernels, body(): pl.pallas_call(hand_out, out_shape=(jax.ShapeDtypeStruct(snr.shape, BF16)...  1.36 us

profile of v4, /device:TPU:0, one launch (start us, length us, event | category | flops | bytes accessed | tf_op | source)
XLA Modules:
  0.0 26.3 jit_solution(12436623265622203945)
XLA Ops:
  0.6 24.3 %detrend_filter.1 = (bf16[4,256,1024]{2,1,0:T(8,128)(2,1)S(1)}, f32[4,256]{1,0:T(4,128)S(1)}) custom-call(s32[4]{0:T(128)} %widths_hbm.1, f32[256,1024]{1,0:T(8,128)} %x_ref.1), custom_call_target="tpu_custom_call" | custom-call | tf_op jit(solution)/shard_map/detrend_filter/pallas_call | solution.py:341
  24.9 1.4 %hand_out.1 = (bf16[4,256,1024]{2,1,0:T(8,128)(2,1)}, f32[4,256]{1,0:T(4,128)}) custom-call(bf16[4,256,1024]{2,1,0:T(8,128)(2,1)S(1)} %get-tuple-element.4.snr_ref, f32[4,256]{1,0:T(4,128)S(1)} %get-tuple-element.5.peaks_ref), custom_call_target="tpu_custom_call" | custom-call | tf_op jit(solution)/shard_map/hand_out/pallas_call | solution.py:378
